TPU v7x, 32 devices: a whole 2x2x4 slice. The times are simulated.
32 devices in a mesh: rows: 16 (over z, y, x), layer: 2 (over core).
Axes of the slice: x: 2, y: 2, z: 4, core: 2. Of those that a mesh axis runs over, the one named last changes fastest.
Arguments:
- grads: bfloat16 [2, 2048, 8192], P('layer', 'rows'), may hold values from -180 to 180
- momentum: float32 [2, 2048, 8192], P('layer', 'rows'), may hold values from -6 to 6
- weights: float32 [2, 2048, 8192], P('layer', 'rows'), may hold values from -1.5 to 1.5
Outputs:
- new_weights: float32 [2, 2048, 8192], P('layer', 'rows')
- new_momentum: float32 [2, 2048, 8192], P('layer', 'rows')
All inputs are finite; a program needn't handle non-finite values.
Results may differ from a plain program's by a relative error of at most 0.0003.
Values sent between devices are 32-bit elements; how exact they have to be, the bound alone decides.
A program may use at most 128 MiB of HBM per device.

v0:
```python
import functools
import math

import jax
import jax.numpy as jnp
from jax import lax
from jax.experimental import pallas as pl
from jax.experimental.pallas import tpu as pltpu
from jax.sharding import PartitionSpec as P

HD = 256
ITERS = 5

coef_a = 3.4445
coef_b = -4.775
coef_c = 2.0315
momentum_decay = 0.95
learn_rate = 0.5
weight_decay = 0.1

HIGHEST = lax.Precision.HIGHEST
MESH = pl.DeviceIdType.MESH


def mm(a, b):
    return jnp.dot(a, b, precision=HIGHEST, preferred_element_type=jnp.float32)


def split(x):
    high = x.astype(jnp.bfloat16)
    low = (x - high.astype(jnp.float32)).astype(jnp.bfloat16)
    return high, low


def polynomial(gram):
    row = lax.broadcasted_iota(jnp.int32, (HD, HD), 0)
    col = lax.broadcasted_iota(jnp.int32, (HD, HD), 1)
    eye = jnp.where(row == col, 1.0, 0.0).astype(jnp.float32)
    trace = jnp.sum(jnp.sum(gram * eye, axis=0, keepdims=True), axis=1, keepdims=True)
    norm = jnp.sqrt(trace) + 1e-07
    a = gram / (norm * norm)
    q = None
    for sweep in range(ITERS):
        p = coef_a * eye + (coef_b * a + coef_c * mm(a, a))
        q = p if q is None else mm(q, p)
        if sweep < ITERS - 1:
            a = mm(mm(a, p), p)
    return q / norm


def pack(x):
    half = HD // 2
    return jnp.stack([x[:half, :half], x[:half, half:], x[half:, half:]])


def unpack(x):
    top = jnp.concatenate([x[0], x[1]], axis=1)
    return jnp.concatenate([top, jnp.concatenate([x[1].T, x[2]], axis=1)], axis=0)


def exchange_kernel(
    plane, devices, layers, limit, scale, g_ref, m_hbm, w_hbm, new_w_ref, new_m_ref,
    m_ref, w_ref, returned, squares, mine, outgoing, held, result, gram_out, grams, own_q, qs,
    square_send, square_recv, out_send, out_recv, back_send, back_recv,
    gram_send, gram_recv, q_send, q_recv, load_sem,
):
    rows = g_ref.shape[0]
    heads = g_ref.shape[1] // HD
    depth = devices // plane
    per_device = heads // devices
    per_plane = heads // plane
    everyone = devices * layers
    me = lax.axis_index("rows")
    layer = lax.axis_index("layer")
    flat = me * layers + layer
    z, p = me // plane, me % plane

    load_m = pltpu.make_async_copy(m_hbm, m_ref, load_sem.at[0])
    load_w = pltpu.make_async_copy(w_hbm, w_ref, load_sem.at[1])
    load_m.start()
    load_w.start()
    barrier = pltpu.get_barrier_semaphore()

    @pl.loop(1, everyone)
    def _(k):
        peer = (flat + k) % everyone
        pl.semaphore_signal(
            barrier, inc=1, device_id={"rows": peer // layers, "layer": peer % layers}, device_id_type=MESH
        )

    def add_squares(h, acc):
        x = g_ref[:, pl.ds(pl.multiple_of(h * HD, HD), HD)].astype(jnp.float32)
        return acc + x * x

    acc = lax.fori_loop(0, heads, add_squares, jnp.zeros((rows, HD), jnp.float32))
    acc = acc.reshape(rows // 8, 8, HD).sum(axis=0)
    part = acc[:, :128] + acc[:, 128:]
    mine[...] = part
    squares[flat] = part
    pl.semaphore_wait(barrier, everyone - 1)

    def square_copy(k):
        peer = (flat + k) % everyone
        return pltpu.make_async_remote_copy(
            src_ref=mine,
            dst_ref=squares.at[flat],
            send_sem=square_send.at[k],
            recv_sem=square_recv.at[k],
            device_id={"rows": peer // layers, "layer": peer % layers},
            device_id_type=MESH,
        )

    @pl.loop(1, everyone)
    def _(k):
        square_copy(k).start()

    @pl.loop(1, everyone)
    def _(k):
        square_copy(k).wait_recv()

    total = jnp.sum(squares[...], axis=0)
    total = jnp.sum(jnp.sum(total, axis=0, keepdims=True), axis=1, keepdims=True)
    factor = jnp.minimum(1.0, limit / (jnp.sqrt(total) + 1e-06))
    load_m.wait()
    load_w.wait()

    def columns_of(h):
        return pl.ds(pl.multiple_of(h * HD, HD), HD)

    def update_of(h):
        clipped = factor * g_ref[:, columns_of(h)].astype(jnp.float32)
        new_momentum = momentum_decay * m_ref[:, columns_of(h)] + clipped
        new_m_ref[:, columns_of(h)] = new_momentum
        return clipped + momentum_decay * new_momentum

    def block(d):
        return pl.ds(pl.multiple_of(d * rows, rows), rows)

    def chunk(j, kz):
        return j * depth + (z + kz) % depth

    def out_copy(j, kz, kp):
        d = (p + kp) % plane
        c = chunk(j, kz)
        return pltpu.make_async_remote_copy(
            src_ref=outgoing.at[d * per_plane + c],
            dst_ref=held.at[c, block(p)],
            send_sem=out_send.at[j, kz, kp],
            recv_sem=out_recv.at[j, kz, kp],
            device_id={"rows": z * plane + d},
            device_id_type=MESH,
        )

    def back_copy(j, kz, kp):
        d = (p + kp) % plane
        c = chunk(j, kz)
        return pltpu.make_async_remote_copy(
            src_ref=result.at[c, block(d)],
            dst_ref=returned.at[p * per_plane + c],
            send_sem=back_send.at[j, kz, kp],
            recv_sem=back_recv.at[j, kz, kp],
            device_id={"rows": z * plane + d},
            device_id_type=MESH,
        )

    def finish(h, ortho):
        w = w_ref[:, columns_of(h)]
        new_w_ref[:, columns_of(h)] = w - learn_rate * (scale * ortho + weight_decay * w)

    def gram_copy(j, kz):
        return pltpu.make_async_remote_copy(
            src_ref=gram_out.at[chunk(j, kz)],
            dst_ref=grams.at[j, z],
            send_sem=gram_send.at[j, kz],
            recv_sem=gram_recv.at[j, kz],
            device_id={"rows": (z + kz) % depth * plane + p},
            device_id_type=MESH,
        )

    def q_copy(j, kz):
        return pltpu.make_async_remote_copy(
            src_ref=own_q.at[j],
            dst_ref=qs.at[j, z],
            send_sem=q_send.at[j, kz],
            recv_sem=q_recv.at[j, kz],
            device_id={"rows": (z + kz) % depth * plane + p},
            device_id_type=MESH,
        )

    def send_update(j):
        @pl.loop(0, depth)
        def _(i):
            kz = (i + 1) % depth
            c = chunk(j, kz)

            @pl.loop(1, plane)
            def _(kp):
                h = (p + kp) % plane * per_plane + c
                outgoing[h] = update_of(h)
                out_copy(j, kz, kp).start()

            held[c, block(p), :] = update_of(p * per_plane + c)

    def send_gram(j):
        @pl.loop(0, depth)
        def _(i):
            kz = (i + 1) % depth

            @pl.loop(1, plane)
            def _(kp):
                out_copy(j, kz, kp).wait_recv()

            x = held[chunk(j, kz)]
            packed = pack(
                lax.dot_general(
                    x, x, (((0,), (0,)), ((), ())), precision=HIGHEST, preferred_element_type=jnp.float32
                )
            )

            @pl.when(kz != 0)
            def _():
                gram_out[chunk(j, kz)] = packed
                gram_copy(j, kz).start()

            @pl.when(kz == 0)
            def _():
                grams[j, z] = packed

    def send_q(j):
        @pl.loop(1, depth)
        def _(kz):
            gram_copy(j, kz).wait_recv()

        packed = pack(polynomial(unpack(jnp.sum(grams[j], axis=0))))
        own_q[j] = packed
        qs[j, z] = packed

        @pl.loop(1, depth)
        def _(kz):
            q_copy(j, kz).start()

    def send_result(j):
        @pl.loop(0, depth)
        def _(i):
            kz = (depth - i) % depth

            @pl.when(i != 0)
            def _():
                q_copy(j, i).wait_recv()

            c = chunk(j, kz)
            q_high, q_low = split(unpack(qs[j, (z + kz) % depth]))
            high, low = split(held[c])
            dot = functools.partial(jnp.dot, preferred_element_type=jnp.float32)
            result[c] = dot(high, q_high) + (dot(high, q_low) + dot(low, q_high))

            @pl.loop(1, plane)
            def _(kp):
                back_copy(j, kz, kp).start()

            finish(p * per_plane + c, result[c, block(p), :])

    for j in range(per_device):
        send_update(j)
    for j in range(per_device):
        send_gram(j)
        if j > 0:
            send_result(j - 1)
        send_q(j)
    send_result(per_device - 1)

    @pl.loop(0, per_device)
    def _(j):
        @pl.loop(0, depth)
        def _(i):
            kz = (depth - i) % depth

            @pl.loop(1, plane)
            def _(kp):
                back_copy(j, kz, kp).wait_recv()
                h = (p + plane - kp) % plane * per_plane + chunk(j, kz)
                finish(h, returned[h])

    @pl.loop(0, per_device)
    def _(j):
        @pl.loop(0, depth)
        def _(kz):
            @pl.loop(1, plane)
            def _(kp):
                back_copy(j, kz, kp).wait_send()
                out_copy(j, kz, kp).wait_send()

        @pl.loop(1, depth)
        def _(kz):
            gram_copy(j, kz).wait_send()
            q_copy(j, kz).wait_send()

    @pl.loop(1, everyone)
    def _(k):
        square_copy(k).wait_send()


def exchange(gradient, momentum, weights, devices, layers, limit, scale):
    rows, width = gradient.shape
    heads = width // HD
    plane = math.gcd(devices, 1 << (devices.bit_length() // 2))
    depth = devices // plane
    per_device = heads // devices
    per_plane = heads // plane
    everyone = devices * layers
    dma = pltpu.SemaphoreType.DMA
    vmem = lambda *shape: pltpu.VMEM(shape, jnp.float32)
    packed = (3, HD // 2, HD // 2)
    return pl.pallas_call(
        functools.partial(exchange_kernel, plane, devices, layers, limit, scale),
        out_shape=(
            jax.ShapeDtypeStruct((rows, width), jnp.float32),
            jax.ShapeDtypeStruct((rows, width), jnp.float32),
        ),
        in_specs=[pl.BlockSpec(memory_space=pltpu.VMEM)] + [pl.BlockSpec(memory_space=pl.ANY)] * 2,
        out_specs=(pl.BlockSpec(memory_space=pltpu.VMEM), pl.BlockSpec(memory_space=pltpu.VMEM)),
        scratch_shapes=[
            vmem(rows, width),
            vmem(rows, width),
            vmem(heads, rows, HD),
            vmem(everyone, 8, 128),
            vmem(8, 128),
            vmem(heads, rows, HD),
            vmem(per_plane, plane * rows, HD),
            vmem(per_plane, plane * rows, HD),
            vmem(per_plane, *packed),
            vmem(per_device, depth, *packed),
            vmem(per_device, *packed),
            vmem(per_device, depth, *packed),
            dma((everyone,)),
            dma((everyone,)),
            dma((per_device, depth, plane)),
            dma((per_device, depth, plane)),
            dma((per_device, depth, plane)),
            dma((per_device, depth, plane)),
            dma((per_device, depth)),
            dma((per_device, depth)),
            dma((per_device, depth)),
            dma((per_device, depth)),
            dma((2,)),
        ],
        compiler_params=pltpu.CompilerParams(
            collective_id=0, has_side_effects=True, vmem_limit_bytes=40 * 1024 * 1024
        ),
    )(gradient, momentum, weights)


def body(grads, momentum, weights):
    devices, layers = lax.axis_size("rows"), lax.axis_size("layer")
    rows, width = grads.shape[1:]
    limit = 0.5 * math.sqrt(float(layers * devices * rows * width))
    scale = 0.2 * math.sqrt(float(max(devices * rows, HD)))
    new_weights, new_momentum = exchange(grads[0], momentum[0], weights[0], devices, layers, limit, scale)
    return (new_weights[None], new_momentum[None])


def shared_body(grads, momentum, weights):
    devices = lax.axis_size("rows")
    rows, width = grads.shape[1:]
    heads = width // HD
    gradient = grads[0].astype(jnp.float32)
    total = lax.psum(jnp.sum(gradient * gradient), ("rows", "layer"))
    limit = 0.5 * math.sqrt(float(lax.axis_size("layer") * devices * rows * width))
    factor = jnp.minimum(1.0, limit / (jnp.sqrt(total) + 1e-06))
    clipped = factor * gradient
    new_momentum = momentum_decay * momentum[0] + clipped
    update = clipped + momentum_decay * new_momentum
    sharers = devices // heads
    part = rows // sharers
    head_major = update.reshape(rows, heads, HD).transpose(1, 0, 2)
    outgoing = jnp.concatenate([head_major] * sharers, axis=0)
    pieces = lax.all_to_all(outgoing, "rows", split_axis=0, concat_axis=1, tiled=True)
    x = pieces[0]
    gram = lax.dot_general(x, x, (((0,), (0,)), ((), ())), precision=HIGHEST)
    result = mm(x, polynomial(gram))
    side = lax.axis_index("rows") // heads
    shares = result.reshape(devices, sharers, part, HD)
    chosen = lax.dynamic_index_in_dim(shares, side, 1, keepdims=False)
    returned = lax.all_to_all(chosen, "rows", split_axis=0, concat_axis=0, tiled=True)
    returned = returned.reshape(sharers, heads, part, HD).transpose(0, 2, 1, 3).reshape(rows, width)
    scale = 0.2 * math.sqrt(float(max(devices * rows, HD)))
    new_weights = weights[0] - learn_rate * (scale * returned + weight_decay * weights[0])
    return (new_weights[None], new_momentum[None])


def solution(mesh):
    placed = P("layer", "rows", None)

    def step(grads, momentum, weights):
        heads = grads.shape[2] // HD
        chosen = body if heads % mesh.shape["rows"] == 0 else shared_body
        return jax.shard_map(
            chosen, mesh=mesh, in_specs=(placed,) * 3, out_specs=(placed, placed), check_vma=False
        )(grads, momentum, weights)

    return step
```

profile of v0, /device:TPU:18, one launch (start us, length us, event | category | flops | bytes accessed | tf_op | source)
XLA Modules:
  0.0 123.7 jit_solution(11376299701919639699)
XLA Ops:
  0.6 0.0 copy-start
  0.6 1.6 %copy-done = bf16[1,128,8192]{2,1,0:T(8,128)(2,1)S(1)} copy-done((bf16[1,128,8192]{2,1,0:T(8,128)(2,1)S(1)}, bf16[1,128,8192]{2,1,0:T(8,128)(2,1)}, u32[]{:S(2)}) %copy-start) | copy-done | bytes 2097176
  2.2 117.5 %shard_map.50 = (f32[128,8192]{1,0:T(8,128)S(1)}, f32[128,8192]{1,0:T(8,128)S(1)}) custom-call(bf16[128,8192]{1,0:T(8,128)(2,1)S(1)} %bitcast.7, f32[128,8192]{1,0:T(8,128)} %bitcast.8, f32[128,8192]{1,0:T(8,128)} %bitcast.9), custom_call_target="tpu_custom_call" | custom-call | tf_op jit(solution)/shard_map/pallas_call | solution.py:314
  119.7 2.0 %copy.7 = f32[1,128,8192]{2,1,0:T(8,128)} copy(f32[1,128,8192]{2,1,0:T(8,128)S(1)} %bitcast.6) | data formatting | bytes 8388608
  121.7 2.0 %copy.8 = f32[1,128,8192]{2,1,0:T(8,128)} copy(f32[1,128,8192]{2,1,0:T(8,128)S(1)} %bitcast.5) | data formatting | bytes 8388608
Async XLA Ops:
  0.6 1.6 %copy-start = (bf16[1,128,8192]{2,1,0:T(8,128)(2,1)S(1)}, bf16[1,128,8192]{2,1,0:T(8,128)(2,1)}, u32[]{:S(2)}) copy-start(bf16[1,128,8192]{2,1,0:T(8,128)(2,1)} %param.3) | copy-start | bytes 6291460
where the time goes:
time: 124 us
  Pallas kernels  117 us (94%)
  local copies, waits for them, and re-layouts  5.61 us (5%)
    pallas_call x1, Pallas kernels, exchange(): pl.pallas_call(functools.partial(exchange_kernel, plane, devices, layers,...  117 us
    unnamed x4, local copies, waits for them, and re-layouts  5.61 us

commit v1 on v0

v1 whole, which is shorter than its diff:
```python
import functools
import math

import jax
import jax.numpy as jnp
from jax import lax
from jax.experimental import pallas as pl
from jax.experimental.pallas import tpu as pltpu
from jax.sharding import PartitionSpec as P

HD = 256
ITERS = 5

coef_a = 3.4445
coef_b = -4.775
coef_c = 2.0315
momentum_decay = 0.95
learn_rate = 0.5
weight_decay = 0.1

HIGHEST = lax.Precision.HIGHEST
MESH = pl.DeviceIdType.MESH


def mm(a, b):
    return jnp.dot(a, b, precision=HIGHEST, preferred_element_type=jnp.float32)


def split(x):
    high = x.astype(jnp.bfloat16)
    low = (x - high.astype(jnp.float32)).astype(jnp.bfloat16)
    return high, low


def polynomial(gram):
    row = lax.broadcasted_iota(jnp.int32, (HD, HD), 0)
    col = lax.broadcasted_iota(jnp.int32, (HD, HD), 1)
    eye = jnp.where(row == col, 1.0, 0.0).astype(jnp.float32)
    trace = jnp.sum(jnp.sum(gram * eye, axis=0, keepdims=True), axis=1, keepdims=True)
    norm = jnp.sqrt(trace) + 1e-07
    a = gram / (norm * norm)
    q = None
    for sweep in range(ITERS):
        p = coef_a * eye + (coef_b * a + coef_c * mm(a, a))
        q = p if q is None else mm(q, p)
        if sweep < ITERS - 1:
            a = mm(mm(a, p), p)
    return q / norm


def dot(a, b):
    return jnp.dot(a, b, preferred_element_type=jnp.float32)


def across(a, b):
    return lax.dot_general(a, b, (((0,), (0,)), ((), ())), preferred_element_type=jnp.float32)


HALF = HD // 2
EDGE = 8
FIRST = HALF + EDGE
PIECES = FIRST + HALF
A = pl.ds(0, FIRST)
B = pl.ds(FIRST, HALF)


def grid_of_half():
    return lax.broadcasted_iota(jnp.int32, (HALF, HALF), 0), lax.broadcasted_iota(jnp.int32, (HALF, HALF), 1)


def store_packed(ref, lower, upper, diagonal, off):
    row, col = grid_of_half()
    ref[pl.ds(0, HALF), :] = jnp.where(row >= col, lower, upper)
    edge = jnp.sum(jnp.where(row == col, diagonal, 0.0), axis=0, keepdims=True)
    ref[pl.ds(HALF, EDGE), :] = jnp.broadcast_to(edge, (EDGE, HALF))
    ref[B, :] = off


def store_gram(ref, x):
    high = x.astype(jnp.bfloat16)
    rest = x - high.astype(jnp.float32)
    middle = rest.astype(jnp.bfloat16)
    low = (rest - middle.astype(jnp.float32)).astype(jnp.bfloat16)
    both = jnp.concatenate([high, middle], axis=0)
    even = across(both, both)
    half = across(jnp.concatenate([high, high], axis=0), jnp.concatenate([middle, low], axis=0))
    row, col = grid_of_half()
    h0, h1 = half[:HALF, :HALF], half[HALF:, HALF:]
    turned = jnp.where(row <= col, h0, h1).T
    e0, e1 = even[:HALF, :HALF], even[HALF:, HALF:]
    off = even[:HALF, HALF:] + (half[:HALF, HALF:] + half[HALF:, :HALF].T)
    store_packed(ref, e0 + h0 + turned, e1 + h1 + turned, e1 + 2.0 * h1, off)


def unpack(ref):
    row, col = grid_of_half()
    block, edge, off = ref[pl.ds(0, HALF), :], ref[pl.ds(HALF, 1), :], ref[B, :]
    turned = block.T
    first = jnp.where(row >= col, block, turned)
    second = jnp.where(row < col, block, jnp.where(row > col, turned, edge))
    return jnp.concatenate(
        [jnp.concatenate([first, off], axis=1), jnp.concatenate([off.T, second], axis=1)], axis=0
    )


def toggle(index, flips, count):
    out, bit = 0, 1
    while bit < count:
        out = out + (index // bit + flips // bit) % 2 * bit
        bit *= 2
    return out


def exchange_kernel(
    devices, layers, limit, scale, g_hbm, m_hbm, w_hbm, new_w_ref, new_m_ref,
    g_ref, m_ref, w_ref, squares, mine, own, ra, ra2, rb, rb2, zr, q,
    square_send, square_recv, a1_send, a1_recv, b1_send, b1_recv, a2_send, a2_recv, b2_send, b2_recv,
    z_send, z_recv, ay_send, ay_recv, ax_send, ax_recv, bx_send, bx_recv, by_send, by_recv,
    qz_send, qz_recv, load_sem,
):
    rows, width = g_ref.shape
    heads = width // HD
    depth = devices // 4
    groups = heads // devices
    everyone = devices * layers
    me = lax.axis_index("rows")
    layer = lax.axis_index("layer")
    flat = me * layers + layer
    z, y, x = me // 4, me // 2 % 2, me % 2
    peer_x = z * 4 + y * 2 + (1 - x)
    peer_y = z * 4 + (1 - y) * 2 + x
    parts = load_sem.shape[0] - 2
    span = width // parts

    def load_g(i):
        cols = pl.ds(i * span, span)
        return pltpu.make_async_copy(g_hbm.at[:, cols], g_ref.at[:, cols], load_sem.at[2 + i])

    load_m = pltpu.make_async_copy(m_hbm, m_ref, load_sem.at[0])
    load_w = pltpu.make_async_copy(w_hbm, w_ref, load_sem.at[1])
    for i in range(parts):
        load_g(i).start()
    load_m.start()
    load_w.start()
    barrier = pltpu.get_barrier_semaphore()

    @pl.loop(1, everyone)
    def _(k):
        peer = (flat + k) % everyone
        pl.semaphore_signal(
            barrier, inc=1, device_id={"rows": peer // layers, "layer": peer % layers}, device_id_type=MESH
        )

    def columns_of(h):
        return pl.ds(pl.multiple_of(h * HD, HD), HD)

    def add_squares(h, acc):
        g = g_ref[:, columns_of(h)].astype(jnp.float32)
        return acc + (g * g).reshape(rows // 8, 8, HD).sum(axis=0)

    acc = jnp.zeros((8, HD), jnp.float32)
    for i in range(parts):
        load_g(i).wait()
        acc = lax.fori_loop(i * (heads // parts), (i + 1) * (heads // parts), add_squares, acc)
    part = acc[:, :128] + acc[:, 128:]
    mine[...] = part
    squares[flat] = part
    pl.semaphore_wait(barrier, everyone - 1)

    def square_copy(k):
        peer = (flat + k) % everyone
        return pltpu.make_async_remote_copy(
            src_ref=mine,
            dst_ref=squares.at[flat],
            send_sem=square_send.at[k],
            recv_sem=square_recv.at[k],
            device_id={"rows": peer // layers, "layer": peer % layers},
            device_id_type=MESH,
        )

    @pl.loop(1, everyone)
    def _(k):
        square_copy(k).start()

    @pl.loop(1, everyone)
    def _(k):
        square_copy(k).wait_recv()

    total = jnp.sum(squares[...], axis=0)
    total = jnp.sum(jnp.sum(total, axis=0, keepdims=True), axis=1, keepdims=True)
    factor = jnp.minimum(1.0, limit / (jnp.sqrt(total) + 1e-06))
    load_m.wait()
    load_w.wait()

    def layer_of(k):
        return toggle(z, k, depth)

    def head_of(j, t, kind):
        owner = t * 4 + (y + kind % 2) % 2 * 2 + (x + kind // 2) % 2
        return owner * groups + j

    def send(src, dst, send_sem, recv_sem, device):
        return pltpu.make_async_remote_copy(
            src_ref=src, dst_ref=dst, send_sem=send_sem, recv_sem=recv_sem,
            device_id={"rows": device}, device_id_type=MESH,
        )

    def a1(j, t, dy):
        return send(own.at[j, t, 2 + dy, A], ra.at[j, t, dy], a1_send.at[j, t, dy], a1_recv.at[j, t, dy], peer_x)

    def b1(j, t, dx):
        return send(own.at[j, t, 2 * dx + 1, B], rb.at[j, t, dx], b1_send.at[j, t, dx], b1_recv.at[j, t, dx], peer_y)

    def a2(j, t):
        return send(own.at[j, t, 1, A], ra2.at[j, t], a2_send.at[j, t], a2_recv.at[j, t], peer_y)

    def b2(j, t):
        return send(own.at[j, t, 2, B], rb2.at[j, t], b2_send.at[j, t], b2_recv.at[j, t], peer_x)

    def zc(j, k):
        t = layer_of(k)
        return send(own.at[j, t, 0], zr.at[j, z], z_send.at[j, k], z_recv.at[j, k], t * 4 + y * 2 + x)

    def qz(j, k):
        t = layer_of(k)
        return send(q.at[j, z, 0], q.at[j, z, 0], qz_send.at[j, k], qz_recv.at[j, k], t * 4 + y * 2 + x)

    def ay(j, t):
        return send(q.at[j, t, 0, A], q.at[j, t, 1, A], ay_send.at[j, t], ay_recv.at[j, t], peer_y)

    def ax(j, t, dy):
        return send(q.at[j, t, dy, A], q.at[j, t, 2 + dy, A], ax_send.at[j, t, dy], ax_recv.at[j, t, dy], peer_x)

    def bx(j, t):
        return send(q.at[j, t, 0, B], q.at[j, t, 2, B], bx_send.at[j, t], bx_recv.at[j, t], peer_x)

    def by(j, t, dx):
        return send(
            q.at[j, t, 2 * dx, B], q.at[j, t, 2 * dx + 1, B], by_send.at[j, t, dx], by_recv.at[j, t, dx], peer_y
        )

    def grams(j, kind):
        for k in reversed(range(depth)):
            t = layer_of(k)
            cols = columns_of(head_of(j, t, kind))
            clipped = factor * g_ref[:, cols].astype(jnp.float32)
            new_momentum = momentum_decay * m_ref[:, cols] + clipped
            new_m_ref[:, cols] = new_momentum
            store_gram(own.at[j, t, kind], clipped + momentum_decay * new_momentum)

    def first_sends(j, kind):
        for k in reversed(range(depth)):
            t = layer_of(k)
            pl.when(kind // 2 == 1)(lambda: a1(j, t, kind % 2).start())
            pl.when(kind % 2 == 1)(lambda: b1(j, t, kind // 2).start())

    def second_send(j, k):
        t = layer_of(k)
        a1(j, t, 1).wait_recv()
        own[j, t, 1, A, :] += ra[j, t, 1]
        a2(j, t).start()
        b1(j, t, 1).wait_recv()
        own[j, t, 2, B, :] += rb[j, t, 1]
        b2(j, t).start()

    def third_send(j, k):
        t = layer_of(k)
        a1(j, t, 0).wait_recv()
        b1(j, t, 0).wait_recv()
        a2(j, t).wait_recv()
        b2(j, t).wait_recv()
        a = own[j, t, 0, A, :] + (ra[j, t, 0] + ra2[j, t])
        b = own[j, t, 0, B, :] + (rb[j, t, 0] + rb2[j, t])
        if k == 0:
            zr[j, t, A, :] = a
            zr[j, t, B, :] = b
        else:
            own[j, t, 0, A, :] = a
            own[j, t, 0, B, :] = b
            zc(j, k).start()

    def solve(j):
        for k in range(1, depth):
            zc(j, k).wait_recv()
        own[j, z, 0] = jnp.sum(zr[j], axis=0)
        p = polynomial(unpack(own.at[j, z, 0]))
        store_packed(q.at[j, z, 0], p[:HALF, :HALF], p[HALF:, HALF:], p[HALF:, HALF:], p[:HALF, HALF:])

    def share(j):
        for k in reversed(range(1, depth)):
            qz(j, k).start()

    def pass_on(j, k):
        t = layer_of(k)
        if not (isinstance(k, int) and k == 0):
            qz(j, k).wait_recv()
        ay(j, t).start()
        bx(j, t).start()
        ax(j, t, 0).start()
        by(j, t, 0).start()

    def pass_far(j, k):
        t = layer_of(k)
        ay(j, t).wait_recv()
        ax(j, t, 1).start()
        bx(j, t).wait_recv()
        by(j, t, 1).start()

    def finish(j, k):
        t = layer_of(k)
        by(j, t, 0).wait_recv()
        by(j, t, 1).wait_recv()
        ax(j, t, 0).wait_recv()
        ax(j, t, 1).wait_recv()
        for kind in range(4):
            cols = columns_of(head_of(j, t, kind))
            q_high, q_low = split(unpack(q.at[j, t, kind]))
            update = factor * g_ref[:, cols].astype(jnp.float32) + momentum_decay * new_m_ref[:, cols]
            high, low = split(update)
            ortho = dot(high, q_high) + (dot(low, q_high) + dot(high, q_low))
            w = w_ref[:, cols]
            new_w_ref[:, cols] = w - learn_rate * (scale * ortho + weight_decay * w)

    def gather(j):
        @pl.loop(0, 4)
        def _(i):
            grams(j, 3 - i)
            first_sends(j, 3 - i)

    def answer(j):
        solve(j)
        share(j)
        pass_on(j, 0)

    last = groups - 1
    far = list(reversed(range(depth)))
    gather(0)
    for j in range(groups):
        for k in far:
            second_send(j, k)
        if j < last:
            gather(j + 1)
        if j > 0:
            answer(j - 1)
        for k in far:
            third_send(j, k)
        if j > 0:
            for k in range(1, depth):
                pass_on(j - 1, k)
                pass_far(j - 1, k - 1)
    answer(last)
    if last > 0:
        for j in range(last):
            pass_far(j, depth - 1)

    @pl.loop(0, depth)
    def _(k):
        @pl.when(k + 1 < depth)
        def _():
            pass_on(last, k + 1)

        pass_far(last, k)
        for j in range(last):
            finish(j, k)

    @pl.loop(0, depth)
    def _(k):
        finish(last, k)

    @pl.loop(0, groups)
    def _(j):
        @pl.loop(0, depth)
        def _(k):
            for c in (a1(j, k, 0), a1(j, k, 1), b1(j, k, 0), b1(j, k, 1), a2(j, k), b2(j, k)):
                c.wait_send()
            for c in (ay(j, k), ax(j, k, 0), ax(j, k, 1), bx(j, k), by(j, k, 0), by(j, k, 1)):
                c.wait_send()

        @pl.loop(1, depth)
        def _(k):
            zc(j, k).wait_send()
            qz(j, k).wait_send()

    @pl.loop(1, everyone)
    def _(k):
        square_copy(k).wait_send()


def exchange(gradient, momentum, weights, devices, layers, limit, scale):
    rows, width = gradient.shape
    heads = width // HD
    depth = devices // 4
    groups = heads // devices
    everyone = devices * layers
    vmem = lambda *shape: pltpu.VMEM(shape, jnp.float32)
    pair = lambda *shape: [pltpu.SemaphoreType.DMA(shape)] * 2
    one, two = (groups, depth), (groups, depth, 2)
    return pl.pallas_call(
        functools.partial(exchange_kernel, devices, layers, limit, scale),
        out_shape=(
            jax.ShapeDtypeStruct((rows, width), jnp.float32),
            jax.ShapeDtypeStruct((rows, width), jnp.float32),
        ),
        in_specs=[pl.BlockSpec(memory_space=pl.ANY)] * 3,
        out_specs=(pl.BlockSpec(memory_space=pltpu.VMEM), pl.BlockSpec(memory_space=pltpu.VMEM)),
        scratch_shapes=[
            pltpu.VMEM((rows, width), gradient.dtype),
            vmem(rows, width),
            vmem(rows, width),
            vmem(everyone, 8, 128),
            vmem(8, 128),
            vmem(groups, depth, 4, PIECES, HALF),
            vmem(groups, depth, 2, FIRST, HALF),
            vmem(groups, depth, FIRST, HALF),
            vmem(groups, depth, 2, HALF, HALF),
            vmem(groups, depth, HALF, HALF),
            vmem(groups, depth, PIECES, HALF),
            vmem(groups, depth, 4, PIECES, HALF),
            *pair(everyone),
            *pair(*two), *pair(*two), *pair(*one), *pair(*one), *pair(*one),
            *pair(*one), *pair(*two), *pair(*one), *pair(*two), *pair(*one),
            pltpu.SemaphoreType.DMA((2 + math.gcd(heads, 4),)),
        ],
        compiler_params=pltpu.CompilerParams(
            collective_id=0, has_side_effects=True, vmem_limit_bytes=56 * 1024 * 1024
        ),
    )(gradient, momentum, weights)


def body(grads, momentum, weights):
    devices, layers = lax.axis_size("rows"), lax.axis_size("layer")
    rows, width = grads.shape[1:]
    limit = 0.5 * math.sqrt(float(layers * devices * rows * width))
    scale = 0.2 * math.sqrt(float(max(devices * rows, HD)))
    new_weights, new_momentum = exchange(grads[0], momentum[0], weights[0], devices, layers, limit, scale)
    return (new_weights[None], new_momentum[None])


def shared_body(grads, momentum, weights):
    devices = lax.axis_size("rows")
    rows, width = grads.shape[1:]
    heads = width // HD
    gradient = grads[0].astype(jnp.float32)
    total = lax.psum(jnp.sum(gradient * gradient), ("rows", "layer"))
    limit = 0.5 * math.sqrt(float(lax.axis_size("layer") * devices * rows * width))
    factor = jnp.minimum(1.0, limit / (jnp.sqrt(total) + 1e-06))
    clipped = factor * gradient
    new_momentum = momentum_decay * momentum[0] + clipped
    update = clipped + momentum_decay * new_momentum
    sharers = devices // heads
    part = rows // sharers
    head_major = update.reshape(rows, heads, HD).transpose(1, 0, 2)
    outgoing = jnp.concatenate([head_major] * sharers, axis=0)
    pieces = lax.all_to_all(outgoing, "rows", split_axis=0, concat_axis=1, tiled=True)
    x = pieces[0]
    gram = lax.dot_general(x, x, (((0,), (0,)), ((), ())), precision=HIGHEST)
    result = mm(x, polynomial(gram))
    side = lax.axis_index("rows") // heads
    shares = result.reshape(devices, sharers, part, HD)
    chosen = lax.dynamic_index_in_dim(shares, side, 1, keepdims=False)
    returned = lax.all_to_all(chosen, "rows", split_axis=0, concat_axis=0, tiled=True)
    returned = returned.reshape(sharers, heads, part, HD).transpose(0, 2, 1, 3).reshape(rows, width)
    scale = 0.2 * math.sqrt(float(max(devices * rows, HD)))
    new_weights = weights[0] - learn_rate * (scale * returned + weight_decay * weights[0])
    return (new_weights[None], new_momentum[None])


def solution(mesh):
    placed = P("layer", "rows", None)

    def step(grads, momentum, weights):
        heads = grads.shape[2] // HD
        devices = mesh.shape["rows"]
        depth = devices // 4
        direct = heads % devices == 0 and devices == 4 * depth and depth & (depth - 1) == 0
        chosen = body if direct else shared_body
        return jax.shard_map(
            chosen, mesh=mesh, in_specs=(placed,) * 3, out_specs=(placed, placed), check_vma=False
        )(grads, momentum, weights)

    return step
```

time: 124 us -> 114 us (0.919)
  the two profiles are of different devices: /device:TPU:18 before, /device:TPU:0 now
where the time goes in v1:
time: 114 us
  Pallas kernels  107 us (94%)
  local copies, waits for them, and re-layouts  6.77 us (6%)
    pallas_call x1, Pallas kernels, exchange(): pl.pallas_call(functools.partial(exchange_kernel, devices, layers, limit,...  107 us
    unnamed x4, local copies, waits for them, and re-layouts  6.77 us

profile of v1, /device:TPU:0, one launch (start us, length us, event | category | flops | bytes accessed | tf_op | source)
XLA Modules:
  0.0 114.0 jit_solution(10133948855223191808)
XLA Ops:
  0.6 106.5 %shard_map.50 = (f32[128,8192]{1,0:T(8,128)}, f32[128,8192]{1,0:T(8,128)}) custom-call(bf16[128,8192]{1,0:T(8,128)(2,1)} %bitcast.9, f32[128,8192]{1,0:T(8,128)} %bitcast.5, f32[128,8192]{1,0:T(8,128)} %bitcast.6), custom_call_target="tpu_custom_call" | custom-call | tf_op jit(solution)/shard_map/pallas_call | solution.py:398
  107.2 0.0 copy-start
  107.2 4.8 %copy.7 = f32[1,128,8192]{2,1,0:T(8,128)} copy(f32[1,128,8192]{2,1,0:T(8,128)} %bitcast.8) | data formatting | bytes 8388608
  111.9 0.0 copy-done
  111.9 2.0 %copy.8 = f32[1,128,8192]{2,1,0:T(8,128)} copy(f32[1,128,8192]{2,1,0:T(8,128)S(1)} %bitcast.7) | data formatting | bytes 8388608
Async XLA Ops:
  107.2 4.8 %copy-start = (f32[128,8192]{1,0:T(8,128)S(1)}, f32[128,8192]{1,0:T(8,128)}, u32[]{:S(2)}) copy-start(f32[128,8192]{1,0:T(8,128)} %get-tuple-element.5) | copy-start | bytes 12582916

commit v2 on v1

--- a/solution.py
+++ b/solution.py
@@ -42,10 +42,17 @@
     q = None
     for sweep in range(ITERS):
         p = coef_a * eye + (coef_b * a + coef_c * mm(a, a))
-        q = p if q is None else mm(q, p)
+        q = p if q is None else near(q, p)
         if sweep < ITERS - 1:
             a = mm(mm(a, p), p)
-    return q / norm
+            yield q
+    yield q / norm
+
+
+def near(a, b):
+    a_high, a_low = split(a)
+    b_high, b_low = split(b)
+    return dot(a_high, b_high) + (dot(a_high, b_low) + dot(a_low, b_high))
 
 
 def dot(a, b):
@@ -101,6 +108,27 @@
     return jnp.concatenate(
         [jnp.concatenate([first, off], axis=1), jnp.concatenate([off.T, second], axis=1)], axis=0
     )
+
+
+def when(condition, action):
+    if isinstance(condition, bool):
+        if condition:
+            action()
+    else:
+        pl.when(condition)(action)
+
+
+def either(condition, first, second):
+    if isinstance(condition, bool):
+        (first if condition else second)()
+    else:
+        pl.when(condition)(first)
+        pl.when(jnp.logical_not(condition))(second)
+
+
+def run(pieces, count):
+    for _ in range(count):
+        next(pieces, None)
 
 
 def toggle(index, flips, count):
@@ -144,12 +172,12 @@
     load_w.start()
     barrier = pltpu.get_barrier_semaphore()
 
-    @pl.loop(1, everyone)
-    def _(k):
-        peer = (flat + k) % everyone
-        pl.semaphore_signal(
-            barrier, inc=1, device_id={"rows": peer // layers, "layer": peer % layers}, device_id_type=MESH
-        )
+    def other(k):
+        peer = lax.rem(flat + k, everyone)
+        return {"rows": lax.div(peer, layers), "layer": lax.rem(peer, layers)}
+
+    for k in range(1, everyone):
+        pl.semaphore_signal(barrier, inc=1, device_id=other(k), device_id_type=MESH)
 
     def columns_of(h):
         return pl.ds(pl.multiple_of(h * HD, HD), HD)
@@ -168,22 +196,18 @@
     pl.semaphore_wait(barrier, everyone - 1)
 
     def square_copy(k):
-        peer = (flat + k) % everyone
         return pltpu.make_async_remote_copy(
             src_ref=mine,
             dst_ref=squares.at[flat],
             send_sem=square_send.at[k],
             recv_sem=square_recv.at[k],
-            device_id={"rows": peer // layers, "layer": peer % layers},
+            device_id=other(k),
             device_id_type=MESH,
         )
 
-    @pl.loop(1, everyone)
-    def _(k):
+    for k in range(1, everyone):
         square_copy(k).start()
-
-    @pl.loop(1, everyone)
-    def _(k):
+    for k in range(1, everyone):
         square_copy(k).wait_recv()
 
     total = jnp.sum(squares[...], axis=0)
@@ -239,20 +263,17 @@
             q.at[j, t, 2 * dx, B], q.at[j, t, 2 * dx + 1, B], by_send.at[j, t, dx], by_recv.at[j, t, dx], peer_y
         )
 
-    def grams(j, kind):
-        for k in reversed(range(depth)):
-            t = layer_of(k)
+    def first_send(j, k):
+        t = layer_of(k)
+        for kind in (3, 2, 1, 0):
             cols = columns_of(head_of(j, t, kind))
             clipped = factor * g_ref[:, cols].astype(jnp.float32)
             new_momentum = momentum_decay * m_ref[:, cols] + clipped
             new_m_ref[:, cols] = new_momentum
             store_gram(own.at[j, t, kind], clipped + momentum_decay * new_momentum)
-
-    def first_sends(j, kind):
-        for k in reversed(range(depth)):
-            t = layer_of(k)
-            pl.when(kind // 2 == 1)(lambda: a1(j, t, kind % 2).start())
-            pl.when(kind % 2 == 1)(lambda: b1(j, t, kind // 2).start())
+        for half in (1, 0):
+            a1(j, t, half).start()
+            b1(j, t, half).start()
 
     def second_send(j, k):
         t = layer_of(k)
@@ -271,24 +292,28 @@
         b2(j, t).wait_recv()
         a = own[j, t, 0, A, :] + (ra[j, t, 0] + ra2[j, t])
         b = own[j, t, 0, B, :] + (rb[j, t, 0] + rb2[j, t])
-        if k == 0:
+
+        def keep():
             zr[j, t, A, :] = a
             zr[j, t, B, :] = b
-        else:
+
+        def pass_up():
             own[j, t, 0, A, :] = a
             own[j, t, 0, B, :] = b
             zc(j, k).start()
+
+        either(k == 0, keep, pass_up)
 
     def solve(j):
         for k in range(1, depth):
             zc(j, k).wait_recv()
         own[j, z, 0] = jnp.sum(zr[j], axis=0)
-        p = polynomial(unpack(own.at[j, z, 0]))
+        for p in polynomial(unpack(own.at[j, z, 0])):
+            yield
         store_packed(q.at[j, z, 0], p[:HALF, :HALF], p[HALF:, HALF:], p[HALF:, HALF:], p[:HALF, HALF:])
-
-    def share(j):
-        for k in reversed(range(1, depth)):
+        for k in range(1, depth):
             qz(j, k).start()
+        pass_on(j, 0)
 
     def pass_on(j, k):
         t = layer_of(k)
@@ -321,47 +346,53 @@
             w = w_ref[:, cols]
             new_w_ref[:, cols] = w - learn_rate * (scale * ortho + weight_decay * w)
 
-    def gather(j):
-        @pl.loop(0, 4)
-        def _(i):
-            grams(j, 3 - i)
-            first_sends(j, 3 - i)
-
-    def answer(j):
-        solve(j)
-        share(j)
-        pass_on(j, 0)
-
     last = groups - 1
-    far = list(reversed(range(depth)))
-    gather(0)
+    steps = groups * depth
+
+    def forward(s):
+        def at(step, action):
+            action(step // depth, depth - 1 - step % depth)
+
+        when(s < steps, lambda: at(s, first_send))
+        when((s >= 1) & (s < steps + 1), lambda: at(s - 1, second_send))
+        when(s >= 2, lambda: at(s - 2, third_send))
+
+    @pl.loop(0, depth + 2)
+    def _(s):
+        forward(s)
+
     for j in range(groups):
-        for k in far:
-            second_send(j, k)
+        pieces = solve(j)
         if j < last:
-            gather(j + 1)
-        if j > 0:
-            answer(j - 1)
-        for k in far:
-            third_send(j, k)
-        if j > 0:
+            for s in range((j + 1) * depth + 2, (j + 2) * depth + 2):
+                run(pieces, 2)
+                forward(s)
+            run(pieces, ITERS + 1)
+        else:
+            if j > 0:
+                for k in range(1, depth):
+                    pass_on(j - 1, k)
+                    pass_far(j - 1, k - 1)
+                    run(pieces, 2)
+            run(pieces, ITERS + 1)
+            if j > 0:
+                pass_far(j - 1, depth - 1)
+        if 0 < j < last:
             for k in range(1, depth):
                 pass_on(j - 1, k)
                 pass_far(j - 1, k - 1)
-    answer(last)
-    if last > 0:
+            pass_far(j - 1, depth - 1)
+
+    @pl.loop(1, depth)
+    def _(k):
+        pass_on(last, k)
+        pass_far(last, k - 1)
         for j in range(last):
-            pass_far(j, depth - 1)
-
-    @pl.loop(0, depth)
-    def _(k):
-        @pl.when(k + 1 < depth)
-        def _():
-            pass_on(last, k + 1)
-
-        pass_far(last, k)
-        for j in range(last):
-            finish(j, k)
+            finish(j, k - 1)
+
+    for j in range(last):
+        finish(j, depth - 1)
+    pass_far(last, depth - 1)
 
     @pl.loop(0, depth)
     def _(k):
@@ -381,8 +412,7 @@
             zc(j, k).wait_send()
             qz(j, k).wait_send()
 
-    @pl.loop(1, everyone)
-    def _(k):
+    for k in range(1, everyone):
         square_copy(k).wait_send()
 
 
@@ -454,7 +484,8 @@
     pieces = lax.all_to_all(outgoing, "rows", split_axis=0, concat_axis=1, tiled=True)
     x = pieces[0]
     gram = lax.dot_general(x, x, (((0,), (0,)), ((), ())), precision=HIGHEST)
-    result = mm(x, polynomial(gram))
+    *_, p = polynomial(gram)
+    result = mm(x, p)
     side = lax.axis_index("rows") // heads
     shares = result.reshape(devices, sharers, part, HD)
     chosen = lax.dynamic_index_in_dim(shares, side, 1, keepdims=False)

time: 114 us -> 109 us (0.956)
  Pallas kernels: 107 us -> 101 us
    pallas_call x1, Pallas kernels: 107 us -> 101 us  [exchange(): pl.pallas_call(functools.partial(exchange_kernel, devices, layers, limit,...]
where the time goes in v2:
time: 109 us
  Pallas kernels  101 us (93%)
  local copies, waits for them, and re-layouts  6.77 us (6%)
    pallas_call x1, Pallas kernels, exchange(): pl.pallas_call(functools.partial(exchange_kernel, devices, layers, limit,...  101 us
    unnamed x4, local copies, waits for them, and re-layouts  6.77 us

profile of v2, /device:TPU:0, one launch (start us, length us, event | category | flops | bytes accessed | tf_op | source)
XLA Modules:
  0.0 108.8 jit_solution(18102526388280059531)
XLA Ops:
  0.6 101.4 %shard_map.50 = (f32[128,8192]{1,0:T(8,128)}, f32[128,8192]{1,0:T(8,128)}) custom-call(bf16[128,8192]{1,0:T(8,128)(2,1)} %bitcast.9, f32[128,8192]{1,0:T(8,128)} %bitcast.5, f32[128,8192]{1,0:T(8,128)} %bitcast.6), custom_call_target="tpu_custom_call" | custom-call | tf_op jit(solution)/shard_map/pallas_call | solution.py:428
  102.1 0.0 copy-start
  102.1 4.8 %copy.7 = f32[1,128,8192]{2,1,0:T(8,128)} copy(f32[1,128,8192]{2,1,0:T(8,128)} %bitcast.8) | data formatting | bytes 8388608
  106.8 0.0 copy-done
  106.8 2.0 %copy.8 = f32[1,128,8192]{2,1,0:T(8,128)} copy(f32[1,128,8192]{2,1,0:T(8,128)S(1)} %bitcast.7) | data formatting | bytes 8388608
Async XLA Ops:
  102.1 4.8 %copy-start = (f32[128,8192]{1,0:T(8,128)S(1)}, f32[128,8192]{1,0:T(8,128)}, u32[]{:S(2)}) copy-start(f32[128,8192]{1,0:T(8,128)} %get-tuple-element.5) | copy-start | bytes 12582916

commit v3 on v2

--- a/solution.py
+++ b/solution.py
@@ -41,10 +41,11 @@
     a = gram / (norm * norm)
     q = None
     for sweep in range(ITERS):
-        p = coef_a * eye + (coef_b * a + coef_c * mm(a, a))
+        p = coef_a * eye + (coef_b * a + coef_c * near(a, a))
         q = p if q is None else near(q, p)
         if sweep < ITERS - 1:
-            a = mm(mm(a, p), p)
+            product = mm if sweep < ITERS - 3 else near
+            a = product(product(a, p), p)
             yield q
     yield q / norm
 
@@ -64,11 +65,18 @@
 
 
 HALF = HD // 2
+PACE = (3, 3)
+EARLY = 2
+EACH = 2
 EDGE = 8
 FIRST = HALF + EDGE
 PIECES = FIRST + HALF
-A = pl.ds(0, FIRST)
-B = pl.ds(FIRST, HALF)
+B = pl.ds(0, HALF)
+A = pl.ds(HALF, HALF + 1)
+BOTH = pl.ds(HALF, HALF)
+LINE = pl.ds(2 * HALF, 1)
+ALL = pl.ds(0, 2 * HALF + 1)
+ONLY_A = pl.ds(0, HALF + 1)
 
 
 def grid_of_half():
@@ -77,9 +85,8 @@
 
 def store_packed(ref, lower, upper, diagonal, off):
     row, col = grid_of_half()
-    ref[pl.ds(0, HALF), :] = jnp.where(row >= col, lower, upper)
-    edge = jnp.sum(jnp.where(row == col, diagonal, 0.0), axis=0, keepdims=True)
-    ref[pl.ds(HALF, EDGE), :] = jnp.broadcast_to(edge, (EDGE, HALF))
+    ref[BOTH, :] = jnp.where(row >= col, lower, upper)
+    ref[LINE, :] = jnp.sum(jnp.where(row == col, diagonal, 0.0), axis=0, keepdims=True)
     ref[B, :] = off
 
 
@@ -101,7 +108,7 @@
 
 def unpack(ref):
     row, col = grid_of_half()
-    block, edge, off = ref[pl.ds(0, HALF), :], ref[pl.ds(HALF, 1), :], ref[B, :]
+    block, edge, off = ref[BOTH, :], ref[LINE, :], ref[B, :]
     turned = block.T
     first = jnp.where(row >= col, block, turned)
     second = jnp.where(row < col, block, jnp.where(row > col, turned, edge))
@@ -230,24 +237,32 @@
         )
 
     def a1(j, t, dy):
-        return send(own.at[j, t, 2 + dy, A], ra.at[j, t, dy], a1_send.at[j, t, dy], a1_recv.at[j, t, dy], peer_x)
+        return send(own.at[j, t, 2 + dy, A], ra.at[j, t, dy, ONLY_A], a1_send.at[j, t, dy], a1_recv.at[j, t, dy], peer_x)
 
     def b1(j, t, dx):
         return send(own.at[j, t, 2 * dx + 1, B], rb.at[j, t, dx], b1_send.at[j, t, dx], b1_recv.at[j, t, dx], peer_y)
 
     def a2(j, t):
-        return send(own.at[j, t, 1, A], ra2.at[j, t], a2_send.at[j, t], a2_recv.at[j, t], peer_y)
+        return send(own.at[j, t, 1, A], ra2.at[j, t, ONLY_A], a2_send.at[j, t], a2_recv.at[j, t], peer_y)
 
     def b2(j, t):
         return send(own.at[j, t, 2, B], rb2.at[j, t], b2_send.at[j, t], b2_recv.at[j, t], peer_x)
 
     def zc(j, k):
         t = layer_of(k)
-        return send(own.at[j, t, 0], zr.at[j, z], z_send.at[j, k], z_recv.at[j, k], t * 4 + y * 2 + x)
-
-    def qz(j, k):
-        t = layer_of(k)
-        return send(q.at[j, z, 0], q.at[j, z, 0], qz_send.at[j, k], qz_recv.at[j, k], t * 4 + y * 2 + x)
+        return send(own.at[j, t, 0, ALL], zr.at[j, z, ALL], z_send.at[j, k], z_recv.at[j, k], t * 4 + y * 2 + x)
+
+    def nearest(i):
+        mirrored = 2 * z >= depth
+        low = jnp.where(mirrored, depth - 1 - z, z)
+        found = jnp.where(i > 2 * low, i, jnp.where(i % 2 == 1, low - (i + 1) // 2, low + i // 2))
+        return jnp.where(mirrored, depth - 1 - found, found)
+
+    def q_up(j, t):
+        return send(q.at[j, t, 0, ALL], q.at[j, t, 0, ALL], qz_send.at[j, t, 0], qz_recv.at[j, t], (me + 4) % devices)
+
+    def q_down(j, t):
+        return send(q.at[j, t, 0, ALL], q.at[j, t, 0, ALL], qz_send.at[j, t, 1], qz_recv.at[j, t], (me + devices - 4) % devices)
 
     def ay(j, t):
         return send(q.at[j, t, 0, A], q.at[j, t, 1, A], ay_send.at[j, t], ay_recv.at[j, t], peer_y)
@@ -271,14 +286,16 @@
             new_momentum = momentum_decay * m_ref[:, cols] + clipped
             new_m_ref[:, cols] = new_momentum
             store_gram(own.at[j, t, kind], clipped + momentum_decay * new_momentum)
-        for half in (1, 0):
-            a1(j, t, half).start()
-            b1(j, t, half).start()
+            if kind == 3:
+                a1(j, t, 1).start()
+                b1(j, t, 1).start()
+        a1(j, t, 0).start()
+        b1(j, t, 0).start()
 
     def second_send(j, k):
         t = layer_of(k)
         a1(j, t, 1).wait_recv()
-        own[j, t, 1, A, :] += ra[j, t, 1]
+        own[j, t, 1, A, :] += ra[j, t, 1, ONLY_A, :]
         a2(j, t).start()
         b1(j, t, 1).wait_recv()
         own[j, t, 2, B, :] += rb[j, t, 1]
@@ -290,7 +307,7 @@
         b1(j, t, 0).wait_recv()
         a2(j, t).wait_recv()
         b2(j, t).wait_recv()
-        a = own[j, t, 0, A, :] + (ra[j, t, 0] + ra2[j, t])
+        a = own[j, t, 0, A, :] + (ra[j, t, 0, ONLY_A, :] + ra2[j, t, ONLY_A, :])
         b = own[j, t, 0, B, :] + (rb[j, t, 0] + rb2[j, t])
 
         def keep():
@@ -307,37 +324,38 @@
     def solve(j):
         for k in range(1, depth):
             zc(j, k).wait_recv()
-        own[j, z, 0] = jnp.sum(zr[j], axis=0)
+        own[j, z, 0, ALL, :] = jnp.sum(zr[j, :, ALL, :], axis=0)
         for p in polynomial(unpack(own.at[j, z, 0])):
             yield
         store_packed(q.at[j, z, 0], p[:HALF, :HALF], p[HALF:, HALF:], p[HALF:, HALF:], p[:HALF, HALF:])
-        for k in range(1, depth):
-            qz(j, k).start()
         pass_on(j, 0)
 
     def pass_on(j, k):
-        t = layer_of(k)
+        t = nearest(k)
         if not (isinstance(k, int) and k == 0):
-            qz(j, k).wait_recv()
+            q_up(j, t).wait_recv()
+        pl.when((z >= t) & (z < depth - 1))(lambda: q_up(j, t).start())
+        pl.when((z <= t) & (z > 0))(lambda: q_down(j, t).start())
         ay(j, t).start()
         bx(j, t).start()
         ax(j, t, 0).start()
         by(j, t, 0).start()
 
     def pass_far(j, k):
-        t = layer_of(k)
+        t = nearest(k)
         ay(j, t).wait_recv()
         ax(j, t, 1).start()
         bx(j, t).wait_recv()
         by(j, t, 1).start()
 
     def finish(j, k):
-        t = layer_of(k)
+        t = nearest(k)
         by(j, t, 0).wait_recv()
-        by(j, t, 1).wait_recv()
         ax(j, t, 0).wait_recv()
-        ax(j, t, 1).wait_recv()
         for kind in range(4):
+            if kind == 3:
+                by(j, t, 1).wait_recv()
+                ax(j, t, 1).wait_recv()
             cols = columns_of(head_of(j, t, kind))
             q_high, q_low = split(unpack(q.at[j, t, kind]))
             update = factor * g_ref[:, cols].astype(jnp.float32) + momentum_decay * new_m_ref[:, cols]
@@ -365,7 +383,7 @@
         pieces = solve(j)
         if j < last:
             for s in range((j + 1) * depth + 2, (j + 2) * depth + 2):
-                run(pieces, 2)
+                run(pieces, EACH)
                 forward(s)
             run(pieces, ITERS + 1)
         else:
@@ -373,7 +391,7 @@
                 for k in range(1, depth):
                     pass_on(j - 1, k)
                     pass_far(j - 1, k - 1)
-                    run(pieces, 2)
+                    run(pieces, PACE[min(k, len(PACE)) - 1])
             run(pieces, ITERS + 1)
             if j > 0:
                 pass_far(j - 1, depth - 1)
@@ -389,12 +407,13 @@
         pass_far(last, k - 1)
         for j in range(last):
             finish(j, k - 1)
+        pl.when(k > EARLY)(lambda: finish(last, k - 1 - EARLY))
 
     for j in range(last):
         finish(j, depth - 1)
     pass_far(last, depth - 1)
 
-    @pl.loop(0, depth)
+    @pl.loop(max(depth - 1 - EARLY, 0), depth)
     def _(k):
         finish(last, k)
 
@@ -407,10 +426,12 @@
             for c in (ay(j, k), ax(j, k, 0), ax(j, k, 1), bx(j, k), by(j, k, 0), by(j, k, 1)):
                 c.wait_send()
 
+            pl.when((z >= k) & (z < depth - 1))(lambda: q_up(j, k).wait_send())
+            pl.when((z <= k) & (z > 0))(lambda: q_down(j, k).wait_send())
+
         @pl.loop(1, depth)
         def _(k):
             zc(j, k).wait_send()
-            qz(j, k).wait_send()
 
     for k in range(1, everyone):
         square_copy(k).wait_send()
@@ -423,7 +444,8 @@
     groups = heads // devices
     everyone = devices * layers
     vmem = lambda *shape: pltpu.VMEM(shape, jnp.float32)
-    pair = lambda *shape: [pltpu.SemaphoreType.DMA(shape)] * 2
+    dma = pltpu.SemaphoreType.DMA
+    pair = lambda *shape: [dma(shape)] * 2
     one, two = (groups, depth), (groups, depth, 2)
     return pl.pallas_call(
         functools.partial(exchange_kernel, devices, layers, limit, scale),
@@ -448,7 +470,7 @@
             vmem(groups, depth, 4, PIECES, HALF),
             *pair(everyone),
             *pair(*two), *pair(*two), *pair(*one), *pair(*one), *pair(*one),
-            *pair(*one), *pair(*two), *pair(*one), *pair(*two), *pair(*one),
+            *pair(*one), *pair(*two), *pair(*one), *pair(*two), dma(two), dma(one),
             pltpu.SemaphoreType.DMA((2 + math.gcd(heads, 4),)),
         ],
         compiler_params=pltpu.CompilerParams(

time: 109 us -> 103 us (0.945)
  Pallas kernels: 101 us -> 95.6 us
    pallas_call x1, Pallas kernels: 101 us -> 95.6 us  [exchange(): pl.pallas_call(functools.partial(exchange_kernel, devices, layers, limit,...]
where the time goes in v3:
time: 103 us
  Pallas kernels  95.6 us (93%)
  local copies, waits for them, and re-layouts  6.77 us (7%)
    pallas_call x1, Pallas kernels, exchange(): pl.pallas_call(functools.partial(exchange_kernel, devices, layers, limit,...  95.6 us
    unnamed x4, local copies, waits for them, and re-layouts  6.77 us

profile of v3, /device:TPU:0, one launch (start us, length us, event | category | flops | bytes accessed | tf_op | source)
XLA Modules:
  0.0 103.0 jit_solution(5902046202940410358)
XLA Ops:
  0.6 95.6 %shard_map.50 = (f32[128,8192]{1,0:T(8,128)}, f32[128,8192]{1,0:T(8,128)}) custom-call(bf16[128,8192]{1,0:T(8,128)(2,1)} %bitcast.9, f32[128,8192]{1,0:T(8,128)} %bitcast.5, f32[128,8192]{1,0:T(8,128)} %bitcast.6), custom_call_target="tpu_custom_call" | custom-call | tf_op jit(solution)/shard_map/pallas_call | solution.py:450
  96.3 0.0 copy-start
  96.3 4.8 %copy.7 = f32[1,128,8192]{2,1,0:T(8,128)} copy(f32[1,128,8192]{2,1,0:T(8,128)} %bitcast.8) | data formatting | bytes 8388608
  101.0 0.0 copy-done
  101.0 2.0 %copy.8 = f32[1,128,8192]{2,1,0:T(8,128)} copy(f32[1,128,8192]{2,1,0:T(8,128)S(1)} %bitcast.7) | data formatting | bytes 8388608
Async XLA Ops:
  96.3 4.8 %copy-start = (f32[128,8192]{1,0:T(8,128)S(1)}, f32[128,8192]{1,0:T(8,128)}, u32[]{:S(2)}) copy-start(f32[128,8192]{1,0:T(8,128)} %get-tuple-element.5) | copy-start | bytes 12582916

commit v4 on v3

--- a/solution.py
+++ b/solution.py
@@ -44,7 +44,7 @@
         p = coef_a * eye + (coef_b * a + coef_c * near(a, a))
         q = p if q is None else near(q, p)
         if sweep < ITERS - 1:
-            product = mm if sweep < ITERS - 3 else near
+            product = mm if sweep < ITERS - 2 else near
             a = product(product(a, p), p)
             yield q
     yield q / norm
@@ -65,7 +65,7 @@
 
 
 HALF = HD // 2
-PACE = (3, 3)
+PACE = (2, 4)
 EARLY = 2
 EACH = 2
 EDGE = 8
@@ -371,8 +371,8 @@
         def at(step, action):
             action(step // depth, depth - 1 - step % depth)
 
+        when((s >= 1) & (s < steps + 1), lambda: at(s - 1, second_send))
         when(s < steps, lambda: at(s, first_send))
-        when((s >= 1) & (s < steps + 1), lambda: at(s - 1, second_send))
         when(s >= 2, lambda: at(s - 2, third_send))
 
     @pl.loop(0, depth + 2)

time: 103 us -> 103 us (level)
  no operation moved by 1% of the time
where the time goes in v4:
time: 103 us
  Pallas kernels  95.4 us (93%)
  local copies, waits for them, and re-layouts  6.77 us (7%)
    pallas_call x1, Pallas kernels, exchange(): pl.pallas_call(functools.partial(exchange_kernel, devices, layers, limit,...  95.4 us
    unnamed x4, local copies, waits for them, and re-layouts  6.77 us

profile of v4, /device:TPU:0, one launch (start us, length us, event | category | flops | bytes accessed | tf_op | source)
XLA Modules:
  0.0 102.9 jit_solution(1710277039660983146)
XLA Ops:
  0.6 95.4 %shard_map.50 = (f32[128,8192]{1,0:T(8,128)}, f32[128,8192]{1,0:T(8,128)}) custom-call(bf16[128,8192]{1,0:T(8,128)(2,1)} %bitcast.9, f32[128,8192]{1,0:T(8,128)} %bitcast.5, f32[128,8192]{1,0:T(8,128)} %bitcast.6), custom_call_target="tpu_custom_call" | custom-call | tf_op jit(solution)/shard_map/pallas_call | solution.py:450
  96.1 0.0 copy-start
  96.1 4.8 %copy.7 = f32[1,128,8192]{2,1,0:T(8,128)} copy(f32[1,128,8192]{2,1,0:T(8,128)} %bitcast.8) | data formatting | bytes 8388608
  100.8 0.0 copy-done
  100.8 2.0 %copy.8 = f32[1,128,8192]{2,1,0:T(8,128)} copy(f32[1,128,8192]{2,1,0:T(8,128)S(1)} %bitcast.7) | data formatting | bytes 8388608
Async XLA Ops:
  96.1 4.8 %copy-start = (f32[128,8192]{1,0:T(8,128)S(1)}, f32[128,8192]{1,0:T(8,128)}, u32[]{:S(2)}) copy-start(f32[128,8192]{1,0:T(8,128)} %get-tuple-element.5) | copy-start | bytes 12582916
